TPU v7x, 256 devices: a whole 4x4x8 slice. The times are simulated.
256 devices in a mesh: gx: 8 (over x_lo, y), gy: 4 (over x_hi, core), gz: 8 (over z).
Axes of the slice: x: 4 (x_hi: 2, x_lo: 2; x = x_hi * 2 + x_lo), y: 4, z: 8, core: 2. Of those that a mesh axis runs over, the one named last changes fastest.
Arguments:
- offsets: float32 [16, 8, 64, 16, 3], P('gx', 'gy', 'gz'), may hold values from 0.2649 to 2.3351, as said below
- velocities: float32 [16, 8, 64, 16, 3], P('gx', 'gy', 'gz'), may hold values from -6 to 6
- occupied: int32 [16, 8, 64, 16], P('gx', 'gy', 'gz'), may hold values 0 or 1
Outputs:
- positions: float32 [16, 8, 64, 16, 3], P('gx', 'gy', 'gz')
- new_velocities: float32 [16, 8, 64, 16, 3], P('gx', 'gy', 'gz')
- forces: float32 [16, 8, 64, 16, 3], P('gx', 'gy', 'gz')
- capacity_history: float32 [4, 2], replicated
Inputs may be any that keep to these rules, and one draw needn't show every extreme that they name: `offsets`: each offset lies within the cell, a jittered body-centred lattice of 16 sites with spacing 1.3 per cell, jitter at most 0.06 in each coordinate.
All inputs are finite; a program needn't handle non-finite values.
Results may differ from a plain program's by a relative error of at most 0.0003.
Values sent between devices are 32-bit elements.
A program may use at most 128 MiB of HBM per device.

v0:
```python
import functools
import itertools

import jax
import jax.numpy as jnp
from jax import lax
from jax.experimental import pallas as pl
from jax.experimental.pallas import tpu as pltpu
from jax.sharding import PartitionSpec as P

MESH = pl.DeviceIdType.MESH
STEPS = 4
CUTOFF = 2.5
CELL_SIDE = 2.6
TIME_STEP = 0.005
BATH_STRENGTH = 0.25
GOAL_WARMTH = 0.8
FORCE_EDGE = 24.0 * (2.0 * CUTOFF ** (-13) - CUTOFF ** (-7))
ENERGY_EDGE = 4.0 * (CUTOFF ** (-12) - CUTOFF ** (-6))
FAR = 32.0
VERLET_VMEM = 60 * 1024 * 1024
UNPACK_VMEM = 4 * 1024 * 1024


NEAR = ("z",)
WIDE = ("xl", "xh", "y")


def parts_of(axes):
    gx, gy, gz = axes
    return {"xl": gx // 4, "y": 4, "xh": gy // 2, "z": gz}


def chips_of(axes, group):
    sizes = parts_of(axes)

    def hops(d):
        return sum(min(o, sizes[a] - o) for a, o in d.items())

    every = itertools.product(*[range(sizes[a]) for a in group])
    return sorted((dict(zip(group, d)) for d in every), key=lambda d: -hops(d))


def offsets_of(size):
    return [0] if size == 1 else [0, 1] if size == 2 else [0, 1, -1]


def canonical(size, off):
    return 0 if size == 1 else off % 2 if size == 2 else off


def padded(size, n):
    return [(canonical(size, -1), n - 1)] + [(0, i) for i in range(n)] + [(canonical(size, 1), 0)]


def partners_of(axes, ny):
    every = itertools.product(*[offsets_of(n) for n in axes])
    flat, rows, found = 0, 0, {}
    for d in every:
        if d == (0, 0, 0):
            continue
        need = sorted({yl for off, yl in padded(axes[1], ny) if off == d[1]})
        if d[2] == 0:
            found[d] = need, flat
            flat += len(need)
        else:
            found[d] = need, rows
            rows += len(need)
    return found, flat, rows


def kernel(
    axes, shape, o_in, v_in, occ_in, result,
    planes_in, kept, ostate, vstate, held, near, osend, orecv, oedge, oedges, vsend, vrecv, vedge, vedges,
    occ_planes, fsend, frecv, fedge, fedges, tally, history, scale, row_sum, near_sums, chip_sum, wide_sums, wide_out,
    in_sem, o_sem, v_sem, f_send_sem, f_recv_sem, near_send, near_recv, wide_send, wide_recv,
):
    gx, gy, gz = axes
    nx, ny, nz, slots = shape
    lanes = nz * slots
    tile = fsend.shape[2]
    slot_total = float(gx * gy * gz * nx * ny * lanes)
    me = [lax.axis_index(a) for a in ("gx", "gy", "gz")]
    sizes = parts_of(axes)
    place = {"xl": me[0] // 4, "y": lax.rem(me[0], 4), "xh": me[1] // 2, "z": me[2]}
    core = lax.rem(me[1], 2)
    leads = core == 1
    follows = core == 0
    near_chips, wide_chips = chips_of(axes, NEAR), chips_of(axes, WIDE)

    turned = [[lax.rem(me[i] + j, n) for j in range(n)] for i, n in enumerate(axes)]

    def device(d):
        return tuple(turned[i][d[i] % axes[i]] for i in range(3))

    def member(d, sign, which):
        at = dict(place)
        for a, o in d.items():
            if o:
                at[a] = lax.rem(at[a] + (o if sign > 0 else sizes[a] - o), sizes[a])
        return (at["xl"] * 4 + at["y"], at["xh"] * 2 + which, at["z"])

    def index_in(group):
        at = 0
        for a in group:
            at = at * sizes[a] + place[a]
        return at

    px_of, py_of = padded(gx, nx), padded(gy, ny)
    xs = offsets_of(gx)
    partners, flats, rows = partners_of(axes, ny)

    def remote(src, dst, send_sem, recv_sem, to):
        return pltpu.make_async_remote_copy(
            src_ref=src, dst_ref=dst, send_sem=send_sem, recv_sem=recv_sem, device_id=to, device_id_type=MESH
        )

    def copies_of(send, recv, edge, edges, send_sem, recv_sem):
        copies = []
        for d, (need, at) in reversed([*partners.items()]):
            where = pl.ds(need[0], len(need))
            to = device(tuple(-x for x in d))
            if d[2] == 0:
                copies.append(remote(send.at[where], recv.at[pl.ds(at, len(need))], send_sem.at[0], recv_sem.at[0], to))
            else:
                src = edge.at[0 if d[2] == 1 else 1, where]
                copies.append(remote(src, edges.at[pl.ds(at, len(need))], send_sem.at[1], recv_sem.at[1], to))
        return copies

    def await_all(ref, sem):
        pltpu.make_async_copy(ref, ref, sem).wait()

    def await_halo(recv, edges, sem):
        await_all(recv, sem.at[0])
        await_all(edges, sem.at[1])

    barrier = pltpu.get_barrier_semaphore()

    greeted = [device(d) for d in partners]
    greeted += [member(d, 1, which) for group in (near_chips, wide_chips) for d in group if any(d.values()) for which in (0, 1)]
    greeted.append(member({}, 1, 1 - core))
    for to in greeted:
        pl.semaphore_signal(barrier, inc=1, device_id=to, device_id_type=MESH)

    loads = [
        pltpu.make_async_copy(o_in, planes_in.at[0], in_sem.at[0]),
        pltpu.make_async_copy(occ_in, occ_planes, in_sem.at[1]),
        pltpu.make_async_copy(v_in, planes_in.at[1], in_sem.at[2]),
    ]
    for load in loads:
        load.start()

    lane = lax.broadcasted_iota(jnp.int32, (nz, lanes), 1)
    level = lax.broadcasted_iota(jnp.int32, (nz, lanes), 0)
    spread = (
        lax.rem(lax.broadcasted_iota(jnp.int32, (slots, lanes), 1), slots)
        == lax.broadcasted_iota(jnp.int32, (slots, lanes), 0)
    ).astype(jnp.float32)

    def rows_of(planes):
        flat = planes.reshape(-1, slots)
        wide = jnp.dot(flat, spread, precision=lax.Precision.HIGHEST, preferred_element_type=jnp.float32)
        wide = wide.reshape(-1, nz, lanes)
        return jnp.sum(jnp.where((lane // slots == level)[None], wide, 0.0), axis=1)

    for load in loads:
        load.wait()
    o_rows = rows_of(planes_in[0])
    v_rows = rows_of(planes_in[1])
    w_rows = rows_of(occ_planes[...].astype(jnp.float32))
    osend[...] = jnp.zeros_like(osend)
    kept[...] = jnp.zeros_like(kept)
    vsend[...] = jnp.zeros_like(vsend)
    fsend[...] = jnp.zeros_like(fsend)
    for x in range(nx):
        for y in range(ny):
            w = w_rows[x * ny + y : x * ny + y + 1]
            for c in range(3):
                i = (x * ny + y) * 3 + c
                r = c * nx + x
                kept[y, r : r + 1] = o_rows[i : i + 1]
                osend[y, r : r + 1] = jnp.where(w > 0.5, o_rows[i : i + 1], FAR)
                vsend[y, r : r + 1] = v_rows[i : i + 1] * w

    quarter = lanes // 4
    row_lane = lane[:1]

    def folded(row, times):
        for i in range(times):
            row = row + pltpu.roll(row, lanes >> (i + 1), 1)
        return row

    tally[...] = folded(jnp.sum(w_rows, axis=0, keepdims=True), 2)

    tile_lane = lax.broadcasted_iota(jnp.int32, (tile, lanes), 1)
    tile_row = lax.broadcasted_iota(jnp.int32, (tile, lanes), 0)
    ends = [lax.rem(tile_lane, slots), lax.rem(tile_lane, slots) + (lanes - slots)]
    back = tile_row * slots + lax.rem(tile_lane, slots)

    def packed(block, side):
        taken = jnp.take_along_axis(block, ends[side], axis=1, mode="promise_in_bounds")
        return jnp.sum(jnp.where(tile_lane // slots == tile_row, taken, 0.0), axis=0, keepdims=True)

    def unpacked(row):
        wide = jnp.broadcast_to(row, (tile, lanes))
        return jnp.take_along_axis(wide, back, axis=1, mode="promise_in_bounds")

    for side in range(2):
        for y in range(ny):
            oedge[side, y] = packed(osend[y], side)
            vedge[side, y] = packed(vsend[y], side)

    pl.semaphore_wait(barrier, len(greeted))
    for copy in copies_of(osend, orecv, oedge, oedges, o_sem.at[0], o_sem.at[1]):
        copy.start()
    for copy in copies_of(vsend, vrecv, vedge, vedges, v_sem.at[0], v_sem.at[1]):
        copy.start()

    def columns(send, recv, edges):
        found = {}
        for xi, a in enumerate(xs):
            for py, (b, yl) in enumerate(py_of):
                if (a, b) == (0, 0):
                    mid = send[yl]
                else:
                    need, at = partners[a, b, 0]
                    mid = recv[at + need.index(yl)]
                ends_of = []
                for c in (-1, 1):
                    need, at = partners[a, b, c]
                    ends_of.append(unpacked(edges[at + need.index(yl)]))
                below, above = ends_of
                found[xi, py, 1] = mid
                low = jnp.where(tile_lane >= lanes - slots, below, mid)
                found[xi, py, 0] = pltpu.roll(low, slots, 1)
                high = jnp.where(tile_lane < slots, above, mid)
                found[xi, py, 2] = pltpu.roll(high, lanes - slots, 1)
        return found

    await_halo(orecv, oedges, o_sem.at[1])
    for (xi, py, dz), value in columns(osend, orecv, oedges).items():
        ostate[xi, py, dz] = value

    lane_id = lax.broadcasted_iota(jnp.int32, (slots, lanes), 1)
    slot_id = lax.broadcasted_iota(jnp.int32, (slots, lanes), 0)
    pick = (lane_id // slots) * slots + slot_id
    itself = lax.rem(lane_id, slots) == slot_id

    def nearby(py):
        for px, (a, xl) in enumerate(px_of):
            for dz in range(3):
                for c in range(3):
                    r = c * nx + xl
                    row = jnp.broadcast_to(ostate[xs.index(a), py, dz, r : r + 1], (slots, lanes))
                    near[px, py, dz, c] = jnp.take_along_axis(row, pick, axis=1, mode="promise_in_bounds")

    half = 0.5 * TIME_STEP
    reach2 = CUTOFF * CUTOFF

    def terms(squared):
        inv = lax.rsqrt(squared)
        inv2 = inv * inv
        inv6 = inv2 * inv2 * inv2
        inv12 = inv6 * inv6
        bond = inv12 - inv6
        return inv, bond, inv * (bond + inv12)

    _, _, edge = terms(jnp.full((slots, lanes), reach2, jnp.float32))
    pair_count = 27.0 * slots

    def step(k, _):
        p = lax.rem(k, 2)
        for py in range(ny + 2):
            nearby(py)

        energy_rows = jnp.zeros((1, lanes), jnp.float32)
        for x in range(nx):
            for y in range(ny):
                block = ostate[0, y + 1, 1]
                mine = [block[c * nx + x : c * nx + x + 1] for c in range(3)]
                occupied = mine[0] < 0.5 * FAR
                force = [jnp.zeros((slots, lanes), jnp.float32) for _ in range(3)]
                bonds, reach = (jnp.zeros((slots, lanes), jnp.float32) for _ in range(2))
                for shift in itertools.product((-1, 0, 1), repeat=3):
                    dx, dy, dz = shift
                    apart = [
                        near[x + 1 + dx, y + 1 + dy, dz + 1, c] - (mine[c] - shift[c] * CELL_SIDE)
                        for c in range(3)
                    ]
                    squared = apart[0] * apart[0] + apart[1] * apart[1] + apart[2] * apart[2]
                    if shift == (0, 0, 0):
                        squared = jnp.where(itself, reach2, squared)
                    squared = jnp.minimum(squared, reach2)
                    inv, bond, push = terms(squared)
                    pull = inv * (edge - push)
                    for c in range(3):
                        force[c] = force[c] + pull * apart[c]
                    bonds = bonds + bond
                    reach = reach + squared * inv
                for c in range(3):
                    total = 24.0 * jnp.sum(force[c], axis=0, keepdims=True)
                    fsend[p, y, c * nx + x : c * nx + x + 1] = jnp.where(occupied, total, 0.0)
                energy = 4.0 * bonds + FORCE_EDGE * reach
                total = jnp.sum(energy, axis=0, keepdims=True)
                total = total - pair_count * (ENERGY_EDGE + CUTOFF * FORCE_EDGE)
                energy_rows = energy_rows + jnp.where(occupied, total, 0.0)

        @pl.when(k > 0)
        def _():
            kinetic = jnp.zeros((tile, lanes), jnp.float32)
            for y in range(ny):
                v = vstate[0, y + 1, 1] + half * fsend[p, y]
                kinetic = kinetic + v * v
            kinetic = folded(jnp.sum(kinetic, axis=0, keepdims=True), 1)
            potential = folded(energy_rows, 2)
            row = jnp.where(
                row_lane < 2 * quarter, 0.5 * kinetic, jnp.where(row_lane < 3 * quarter, 0.5 * potential, tally[...])
            )
            row_sum[...] = row
            at = index_in(NEAR) * 2 + core
            for d in near_chips:
                if any(d.values()):
                    remote(row_sum, near_sums.at[p, at], near_send, near_recv.at[p], member(d, -1, 1)).start()

            @pl.when(follows)
            def _():
                remote(row_sum, near_sums.at[p, at], near_send, near_recv.at[p], member({}, 1, 1)).start()

            @pl.when(leads)
            def _():
                near_sums[p, at] = row

        @pl.when(k < STEPS)
        def _():
            for side in range(2):
                for y in range(ny):
                    fedge[p, side, y] = packed(fsend[p, y], side)
            for copy in copies_of(
                fsend.at[p], frecv.at[p], fedge.at[p], fedges.at[p], f_send_sem, f_recv_sem.at[p]
            ):
                copy.start()

        def total_of(ref, n):
            parts = [ref[p, i] for i in range(n)]
            while len(parts) > 1:
                parts = [sum(parts[i + 1 : i + 2], parts[i]) for i in range(0, len(parts), 2)]
            return parts[0]

        n_near, n_wide = len(near_chips), len(wide_chips)

        @pl.when((k > 0) & leads)
        def _():
            await_all(near_sums.at[p, pl.ds(0, 2 * n_near - 1)], near_recv.at[p])
            row = total_of(near_sums, 2 * n_near)
            chip_sum[...] = row
            at = index_in(WIDE)
            for d in wide_chips:
                for which in (0, 1):
                    if which == 0 or any(d.values()):
                        remote(
                            chip_sum, wide_sums.at[p, at], wide_send, wide_recv.at[p], member(d, -1, which)
                        ).start()
            wide_sums[p, at] = row

        @pl.when(k == 0)
        def _():
            await_halo(vrecv, vedges, v_sem.at[1])
            for (xi, py, dz), value in columns(vsend, vrecv, vedges).items():
                vstate[xi, py, dz] = value

        @pl.when(k < STEPS)
        def _():
            await_halo(frecv.at[p], fedges.at[p], f_recv_sem.at[p])
            await_halo(frecv.at[p], fedges.at[p], f_send_sem)
            before = jnp.where(k > 0, half, 0.0)
            for (xi, py, dz), f in columns(fsend.at[p], frecv.at[p], fedges.at[p]).items():
                vstate[xi, py, dz] = vstate[xi, py, dz] + before * f
                held[xi, py, dz] = half * f

        @pl.when(k > 0)
        def _():
            @pl.when(leads)
            def _():
                await_all(near_sums.at[p, pl.ds(0, n_near - 1)], near_send)
                await_all(wide_sums.at[p, pl.ds(0, n_wide - 1)], wide_recv.at[p])

            @pl.when(follows)
            def _():
                await_all(near_sums.at[p, pl.ds(0, n_near)], near_send)
                await_all(wide_sums.at[p], wide_recv.at[p])

            row = total_of(wide_sums, n_wide)

            def across(low, high):
                picked = jnp.where((row_lane >= low * quarter) & (row_lane < high * quarter), row, 0.0)
                return jnp.broadcast_to(jnp.sum(picked, axis=1, keepdims=True), (1, lanes))

            vigor, potential, count = across(0, 2), across(2, 3), across(3, 4)
            square = (1.0 - BATH_STRENGTH) + (BATH_STRENGTH * GOAL_WARMTH * 1.5) * count / vigor
            which = lax.broadcasted_iota(jnp.int32, (2, lanes), 1)
            record = jnp.concatenate([potential, square * vigor], axis=0) / slot_total
            history[...] = jnp.where(which == k - 1, record, history[...])
            scale[...] = jnp.sqrt(square)

            @pl.when(leads)
            def _():
                await_all(wide_out, wide_send)

        lam = scale[...]

        @pl.when(k < STEPS)
        def _():
            for xi in range(len(xs)):
                for py in range(ny + 2):
                    for dz in range(3):
                        v = vstate[xi, py, dz] * lam + held[xi, py, dz]
                        vstate[xi, py, dz] = v
                        ostate[xi, py, dz] = ostate[xi, py, dz] + TIME_STEP * v

        @pl.when(k == STEPS)
        def _():
            for y in range(ny):
                here = ostate[0, y + 1, 1]
                result[y] = jnp.where(here < 0.5 * FAR, here, kept[y])
                result[ny + y] = (vstate[0, y + 1, 1] + half * fsend[p, y]) * lam
                result[2 * ny + y] = fsend[p, y]
            result[3 * ny, 0:2] = history[...]

        return 0

    history[...] = jnp.zeros_like(history)
    scale[...] = jnp.ones_like(scale)
    lax.fori_loop(0, STEPS + 1, step, 0)
    await_halo(orecv, oedges, o_sem.at[0])
    await_halo(vrecv, vedges, v_sem.at[0])


def unpack(shape, result, o_out, v_out, f_out, h_out):
    nx, ny, nz, slots = shape
    lanes = nz * slots
    at = lax.broadcasted_iota(jnp.int32, (nz, lanes), 0) * slots + lax.rem(
        lax.broadcasted_iota(jnp.int32, (nz, lanes), 1), slots
    )
    for i, ref in enumerate((o_out, v_out, f_out)):
        for y in range(ny):
            for x in range(nx):
                for c in range(3):
                    r = c * nx + x
                    row = jnp.broadcast_to(result[i * ny + y, r : r + 1], (nz, lanes))
                    ref[x, y, c] = jnp.take_along_axis(row, at, axis=1, mode="promise_in_bounds")[:, :slots]
    h_out[...] = result[3 * ny, 0:2, :STEPS]


def shards(axes, offsets, velocities, occupied):
    nx, ny, nz, slots = occupied.shape
    lanes = nz * slots
    tile = lanes // slots
    assert axes[2] > 2 and tile >= 3 * nx
    _, flats, rows = partners_of(axes, ny)
    nxo = len(offsets_of(axes[0]))
    n_near, n_wide = (len(chips_of(axes, group)) for group in (NEAR, WIDE))
    f32 = jnp.float32
    plane = jax.ShapeDtypeStruct((nx, ny, 3, nz, slots), f32)
    vmem = pl.BlockSpec(memory_space=pltpu.VMEM)
    dma = pltpu.SemaphoreType.DMA
    state = pltpu.VMEM((nxo, ny + 2, 3, tile, lanes), f32)
    halo = [
        pltpu.VMEM((ny, tile, lanes), f32),
        pltpu.VMEM((flats, tile, lanes), f32),
        pltpu.VMEM((2, ny, 1, lanes), f32),
        pltpu.VMEM((rows, 1, lanes), f32),
    ]
    result = pl.pallas_call(
        functools.partial(kernel, axes, (nx, ny, nz, slots)),
        name="verlet",
        out_shape=pltpu.VMEM((3 * ny + 1, tile, lanes), f32),
        in_specs=[pl.BlockSpec(memory_space=pltpu.HBM)] * 3,
        out_specs=vmem,
        scratch_shapes=[
            pltpu.VMEM((2, nx, ny, 3, nz, slots), f32),
            pltpu.VMEM((ny, tile, lanes), f32),
            state,
            state,
            state,
            pltpu.VMEM((nx + 2, ny + 2, 3, 3, slots, lanes), f32),
            *halo,
            *halo,
            pltpu.VMEM((nx, ny, nz, slots), jnp.int32),
            pltpu.VMEM((2, ny, tile, lanes), f32),
            pltpu.VMEM((2, flats, tile, lanes), f32),
            pltpu.VMEM((2, 2, ny, 1, lanes), f32),
            pltpu.VMEM((2, rows, 1, lanes), f32),
            pltpu.VMEM((1, lanes), f32),
            pltpu.VMEM((2, lanes), f32),
            pltpu.VMEM((1, lanes), f32),
            pltpu.VMEM((1, lanes), f32),
            pltpu.VMEM((2, 2 * n_near, 1, lanes), f32),
            pltpu.VMEM((1, lanes), f32),
            pltpu.VMEM((2, n_wide, 1, lanes), f32),
            pltpu.VMEM((2 * n_wide - 1, 1, lanes), f32),
            dma((3,)),
            dma((2, 2)),
            dma((2, 2)),
            dma((2,)),
            dma((2, 2)),
            dma,
            dma((2,)),
            dma,
            dma((2,)),
        ],
        compiler_params=pltpu.CompilerParams(
            collective_id=0, has_side_effects=True, vmem_limit_bytes=VERLET_VMEM
        ),
    )(
        jnp.transpose(offsets, (0, 1, 4, 2, 3)),
        jnp.transpose(velocities, (0, 1, 4, 2, 3)),
        occupied,
    )
    o, v, f, h = pl.pallas_call(
        functools.partial(unpack, (nx, ny, nz, slots)),
        name="unpack",
        out_shape=[plane, plane, plane, jax.ShapeDtypeStruct((2, STEPS), f32)],
        in_specs=[vmem],
        out_specs=[vmem] * 4,
        compiler_params=pltpu.CompilerParams(vmem_limit_bytes=UNPACK_VMEM),
    )(result)
    back = (0, 1, 3, 4, 2)
    return (jnp.transpose(o, back), jnp.transpose(v, back), jnp.transpose(f, back), h.T)


def solution(mesh):
    axes = tuple(mesh.shape[a] for a in ("gx", "gy", "gz"))
    in_specs = (
        P("gx", "gy", "gz", None, None),
        P("gx", "gy", "gz", None, None),
        P("gx", "gy", "gz", None),
    )
    out_specs = (
        P("gx", "gy", "gz", None, None),
        P("gx", "gy", "gz", None, None),
        P("gx", "gy", "gz", None, None),
        P(),
    )
    return jax.shard_map(
        functools.partial(shards, axes), mesh=mesh, in_specs=in_specs, out_specs=out_specs, check_vma=False
    )
```

profile of v0, /device:TPU:1, one launch (start us, length us, event | category | flops | bytes accessed | tf_op | source)
XLA Modules:
  0.0 61.3 jit_solution(885444290959372900)
XLA Ops:
  0.6 60.0 %verlet.1.result = f32[7,8,128]{2,1,0:T(8,128)S(1)} custom-call(f32[2,2,3,8,16]{4,3,2,1,0:T(8,128)} %bitcast.6, f32[2,2,3,8,16]{4,3,2,1,0:T(8,128)} %bitcast.7, s32[2,2,8,16]{3,2,1,0:T(8,128)} %occ_in.1), custom_call_target="tpu_custom_call" | custom-call | tf_op jit(solution)/shard_map/verlet/pallas_call | solution.py:473
  60.6 0.7 %unpack.1 = (f32[2,2,3,8,16]{4,3,2,1,0:T(8,128)}, f32[2,2,3,8,16]{4,3,2,1,0:T(8,128)}, f32[2,2,3,8,16]{4,3,2,1,0:T(8,128)}, f32[2,4]{1,0:T(2,128)}) custom-call(f32[7,8,128]{2,1,0:T(8,128)S(1)} %verlet.1.result), custom_call_target="tpu_custom_call" | custom-call | tf_op jit(solution)/shard_map/unpack/pallas_call | solution.py:519
where the time goes:
time: 61.5 us; the launch traced here: 61.3 us
  Pallas kernels  60.7 us (99%)
  between operations  0.64 us (1%)
    pallas_call x1, Pallas kernels, shards(): pl.pallas_call(functools.partial(kernel, axes, (nx, ny, nz, slots)), name...  60 us

commit v1 on v0

--- a/solution.py
+++ b/solution.py
@@ -51,6 +51,25 @@
 
 def padded(size, n):
     return [(canonical(size, -1), n - 1)] + [(0, i) for i in range(n)] + [(canonical(size, 1), 0)]
+
+
+def deep(size, n):
+    low, high = canonical(size, -1), canonical(size, 1)
+    return [(low, n - 2), (low, n - 1)] + [(0, i) for i in range(n)] + [(high, 0), (high, 1)]
+
+
+def deep_places(axes, ny):
+    flat, rows, found = 0, 0, {}
+    for d in itertools.product(*[offsets_of(n) for n in axes]):
+        if d == (0, 0, 0):
+            continue
+        if d[2] == 0:
+            found[d] = flat
+            flat += ny
+        else:
+            found[d] = rows
+            rows += 2 * ny
+    return found, flat, rows
 
 
 def partners_of(axes, ny):
@@ -71,8 +90,8 @@
 
 def kernel(
     axes, shape, o_in, v_in, occ_in, result,
-    planes_in, kept, ostate, vstate, held, near, osend, orecv, oedge, oedges, vsend, vrecv, vedge, vedges,
-    occ_planes, fsend, frecv, fedge, fedges, tally, history, scale, row_sum, near_sums, chip_sum, wide_sums, wide_out,
+    planes_in, kept, ostate, vstate, held, near, around, first_near, first_force, osend, orecv, oedge, oedges, vsend, vrecv, vedge, vedges,
+    occ_planes, fsend, frecv, fedge, fedges, tally, history, row_sum, near_sums, chip_sum, wide_sums, wide_out,
     in_sem, o_sem, v_sem, f_send_sem, f_recv_sem, near_send, near_recv, wide_send, wide_recv,
 ):
     gx, gy, gz = axes
@@ -194,11 +213,12 @@
 
     tile_lane = lax.broadcasted_iota(jnp.int32, (tile, lanes), 1)
     tile_row = lax.broadcasted_iota(jnp.int32, (tile, lanes), 0)
-    ends = [lax.rem(tile_lane, slots), lax.rem(tile_lane, slots) + (lanes - slots)]
+    slot_lane = lax.rem(tile_lane, slots)
+    ends = [[slot_lane + (i if side == 0 else nz - 1 - i) * slots for i in range(2)] for side in range(2)]
     back = tile_row * slots + lax.rem(tile_lane, slots)
 
-    def packed(block, side):
-        taken = jnp.take_along_axis(block, ends[side], axis=1, mode="promise_in_bounds")
+    def packed(block, side, depth=0):
+        taken = jnp.take_along_axis(block, ends[side][depth], axis=1, mode="promise_in_bounds")
         return jnp.sum(jnp.where(tile_lane // slots == tile_row, taken, 0.0), axis=0, keepdims=True)
 
     def unpacked(row):
@@ -207,12 +227,19 @@
 
     for side in range(2):
         for y in range(ny):
-            oedge[side, y] = packed(osend[y], side)
+            for depth in range(2):
+                oedge[side, 2 * y + depth] = packed(osend[y], side, depth)
             vedge[side, y] = packed(vsend[y], side)
 
     pl.semaphore_wait(barrier, len(greeted))
-    for copy in copies_of(osend, orecv, oedge, oedges, o_sem.at[0], o_sem.at[1]):
-        copy.start()
+    places, _, _ = deep_places(axes, ny)
+    for d, at in reversed([*places.items()]):
+        to = device(tuple(-x for x in d))
+        if d[2] == 0:
+            remote(osend, orecv.at[pl.ds(at, ny)], o_sem.at[0, 0], o_sem.at[1, 0], to).start()
+        else:
+            src = oedge.at[0 if d[2] == 1 else 1]
+            remote(src, oedges.at[pl.ds(at, 2 * ny)], o_sem.at[0, 1], o_sem.at[1, 1], to).start()
     for copy in copies_of(vsend, vrecv, vedge, vedges, v_sem.at[0], v_sem.at[1]):
         copy.start()
 
@@ -237,9 +264,44 @@
                 found[xi, py, 2] = pltpu.roll(high, lanes - slots, 1)
         return found
 
+    cell = tile_lane // slots
+    deep_x, deep_y = deep(gx, nx), deep(gy, ny)
+    pairs = ny + 2
+
+    def neighbourhood():
+        ends_of = {}
+        for xi, a in enumerate(xs):
+            for at, (b, yl) in enumerate(deep_y):
+                mid = osend[yl] if (a, b) == (0, 0) else orecv[places[a, b, 0] + yl]
+                below, above = (
+                    [unpacked(oedges[places[a, b, c] + 2 * yl + depth]) for depth in range(2)] for c in (-1, 1)
+                )
+                low = jnp.where(tile_lane >= lanes - slots, below[0], mid)
+                high = jnp.where(tile_lane < slots, above[0], mid)
+                around[xi, at, 0] = pltpu.roll(low, slots, 1)
+                around[xi, at, 1] = mid
+                around[xi, at, 2] = pltpu.roll(high, lanes - slots, 1)
+                bottom = jnp.where(cell == 0, below[1], jnp.where(cell == 1, below[0], pltpu.roll(mid, 2 * slots, 1)))
+                top = jnp.where(cell == nz - 1, above[1], above[0])
+                top = jnp.where(cell == nz - 3, pltpu.roll(mid, lanes - 2 * slots, 1), top)
+                ends_of[xi, at] = jnp.where(cell < nz // 2, bottom, top)
+        for xi in range(len(xs)):
+            for dy in range(3):
+                for dz in range(3):
+                    centre = jnp.where(lax.rem(cell, 2) == 0, dz, nz - 3 + dz)
+                    source = centre * slots + slot_lane
+                    gathered = jnp.zeros((tile, lanes), jnp.float32)
+                    for t in range(pairs):
+                        taken = jnp.take_along_axis(ends_of[xi, t + dy], source, axis=1, mode="promise_in_bounds")
+                        gathered = jnp.where(cell // 2 == t, taken, gathered)
+                    around[xi, pairs + 2 + dy, dz] = gathered
+
     await_halo(orecv, oedges, o_sem.at[1])
-    for (xi, py, dz), value in columns(osend, orecv, oedges).items():
-        ostate[xi, py, dz] = value
+    neighbourhood()
+    for xi in range(len(xs)):
+        for py in range(ny + 2):
+            for dz in range(3):
+                ostate[xi, py, dz] = around[xi, py + 1, dz]
 
     lane_id = lax.broadcasted_iota(jnp.int32, (slots, lanes), 1)
     slot_id = lax.broadcasted_iota(jnp.int32, (slots, lanes), 0)
@@ -268,6 +330,63 @@
     _, _, edge = terms(jnp.full((slots, lanes), reach2, jnp.float32))
     pair_count = 27.0 * slots
 
+    def pair_sums(mine, near_of):
+        force = [jnp.zeros((slots, lanes), jnp.float32) for _ in range(3)]
+        bonds, reach = (jnp.zeros((slots, lanes), jnp.float32) for _ in range(2))
+        for shift in itertools.product((-1, 0, 1), repeat=3):
+            apart = [near_of(shift, c) - (mine[c] - shift[c] * CELL_SIDE) for c in range(3)]
+            squared = apart[0] * apart[0] + apart[1] * apart[1] + apart[2] * apart[2]
+            if shift == (0, 0, 0):
+                squared = jnp.where(itself, reach2, squared)
+            squared = jnp.minimum(squared, reach2)
+            inv, bond, push = terms(squared)
+            pull = inv * (edge - push)
+            for c in range(3):
+                force[c] = force[c] + pull * apart[c]
+            bonds = bonds + bond
+            reach = reach + squared * inv
+        return [24.0 * jnp.sum(f, axis=0, keepdims=True) for f in force], bonds, reach
+
+    def first_row(i, _):
+        centre = i + 1 + 2 * (i // pairs)
+        for px, (a, xl) in enumerate(deep_x):
+            for dy in range(3):
+                for dz in range(3):
+                    for c in range(3):
+                        r = c * nx + xl
+                        row = jnp.broadcast_to(around[xs.index(a), centre - 1 + dy, dz, r : r + 1], (slots, lanes))
+                        first_near[px, dy, dz, c] = jnp.take_along_axis(row, pick, axis=1, mode="promise_in_bounds")
+        for px, (a, xl) in enumerate(px_of):
+            block = around[xs.index(a), centre, 1]
+            mine = [block[c * nx + xl : c * nx + xl + 1] for c in range(3)]
+            force, _, _ = pair_sums(
+                mine, lambda shift, c: first_near[px + 1 + shift[0], 1 + shift[1], 1 + shift[2], c]
+            )
+            for c in range(3):
+                r = c * nx + xl
+                first_force[xs.index(a), i, r : r + 1] = jnp.where(mine[0] < 0.5 * FAR, force[c], 0.0)
+        return 0
+
+    first_force[...] = jnp.zeros_like(first_force)
+    lax.fori_loop(0, pairs + 1, first_row, 0)
+
+    await_halo(vrecv, vedges, v_sem.at[1])
+    first_v = columns(vsend, vrecv, vedges)
+    for xi in range(len(xs)):
+        outer = first_force[xi, pairs]
+        for py in range(pairs):
+            mid = first_force[xi, py]
+            low = jnp.where(tile_lane < slots, pltpu.roll(outer, (lanes - 2 * py * slots) % lanes, 1), pltpu.roll(mid, slots, 1))
+            high = jnp.where(
+                tile_lane >= lanes - slots,
+                pltpu.roll(outer, lanes - 2 * (py + 1) * slots, 1),
+                pltpu.roll(mid, lanes - slots, 1),
+            )
+            for dz, f in enumerate((low, mid, high)):
+                v = first_v[xi, py, dz] + half * f
+                vstate[xi, py, dz] = v
+                ostate[xi, py, dz] = ostate[xi, py, dz] + TIME_STEP * v
+
     def step(k, _):
         p = lax.rem(k, 2)
         for py in range(ny + 2):
@@ -279,56 +398,39 @@
                 block = ostate[0, y + 1, 1]
                 mine = [block[c * nx + x : c * nx + x + 1] for c in range(3)]
                 occupied = mine[0] < 0.5 * FAR
-                force = [jnp.zeros((slots, lanes), jnp.float32) for _ in range(3)]
-                bonds, reach = (jnp.zeros((slots, lanes), jnp.float32) for _ in range(2))
-                for shift in itertools.product((-1, 0, 1), repeat=3):
-                    dx, dy, dz = shift
-                    apart = [
-                        near[x + 1 + dx, y + 1 + dy, dz + 1, c] - (mine[c] - shift[c] * CELL_SIDE)
-                        for c in range(3)
-                    ]
-                    squared = apart[0] * apart[0] + apart[1] * apart[1] + apart[2] * apart[2]
-                    if shift == (0, 0, 0):
-                        squared = jnp.where(itself, reach2, squared)
-                    squared = jnp.minimum(squared, reach2)
-                    inv, bond, push = terms(squared)
-                    pull = inv * (edge - push)
-                    for c in range(3):
-                        force[c] = force[c] + pull * apart[c]
-                    bonds = bonds + bond
-                    reach = reach + squared * inv
+                force, bonds, reach = pair_sums(
+                    mine, lambda shift, c: near[x + 1 + shift[0], y + 1 + shift[1], 1 + shift[2], c]
+                )
                 for c in range(3):
-                    total = 24.0 * jnp.sum(force[c], axis=0, keepdims=True)
-                    fsend[p, y, c * nx + x : c * nx + x + 1] = jnp.where(occupied, total, 0.0)
+                    r = c * nx + x
+                    fsend[p, y, r : r + 1] = jnp.where(occupied, force[c], 0.0)
                 energy = 4.0 * bonds + FORCE_EDGE * reach
                 total = jnp.sum(energy, axis=0, keepdims=True)
                 total = total - pair_count * (ENERGY_EDGE + CUTOFF * FORCE_EDGE)
                 energy_rows = energy_rows + jnp.where(occupied, total, 0.0)
 
-        @pl.when(k > 0)
-        def _():
-            kinetic = jnp.zeros((tile, lanes), jnp.float32)
-            for y in range(ny):
-                v = vstate[0, y + 1, 1] + half * fsend[p, y]
-                kinetic = kinetic + v * v
-            kinetic = folded(jnp.sum(kinetic, axis=0, keepdims=True), 1)
-            potential = folded(energy_rows, 2)
-            row = jnp.where(
-                row_lane < 2 * quarter, 0.5 * kinetic, jnp.where(row_lane < 3 * quarter, 0.5 * potential, tally[...])
-            )
-            row_sum[...] = row
-            at = index_in(NEAR) * 2 + core
-            for d in near_chips:
-                if any(d.values()):
-                    remote(row_sum, near_sums.at[p, at], near_send, near_recv.at[p], member(d, -1, 1)).start()
-
-            @pl.when(follows)
-            def _():
-                remote(row_sum, near_sums.at[p, at], near_send, near_recv.at[p], member({}, 1, 1)).start()
-
-            @pl.when(leads)
-            def _():
-                near_sums[p, at] = row
+        kinetic = jnp.zeros((tile, lanes), jnp.float32)
+        for y in range(ny):
+            v = vstate[0, y + 1, 1] + half * fsend[p, y]
+            kinetic = kinetic + v * v
+        kinetic = folded(jnp.sum(kinetic, axis=0, keepdims=True), 1)
+        potential = folded(energy_rows, 2)
+        row = jnp.where(
+            row_lane < 2 * quarter, 0.5 * kinetic, jnp.where(row_lane < 3 * quarter, 0.5 * potential, tally[...])
+        )
+        row_sum[...] = row
+        at = index_in(NEAR) * 2 + core
+        for d in near_chips:
+            if any(d.values()):
+                remote(row_sum, near_sums.at[p, at], near_send, near_recv.at[p], member(d, -1, 1)).start()
+
+        @pl.when(follows)
+        def _():
+            remote(row_sum, near_sums.at[p, at], near_send, near_recv.at[p], member({}, 1, 1)).start()
+
+        @pl.when(leads)
+        def _():
+            near_sums[p, at] = row
 
         @pl.when(k < STEPS)
         def _():
@@ -348,7 +450,7 @@
 
         n_near, n_wide = len(near_chips), len(wide_chips)
 
-        @pl.when((k > 0) & leads)
+        @pl.when(leads)
         def _():
             await_all(near_sums.at[p, pl.ds(0, 2 * n_near - 1)], near_recv.at[p])
             row = total_of(near_sums, 2 * n_near)
@@ -362,51 +464,41 @@
                         ).start()
             wide_sums[p, at] = row
 
-        @pl.when(k == 0)
-        def _():
-            await_halo(vrecv, vedges, v_sem.at[1])
-            for (xi, py, dz), value in columns(vsend, vrecv, vedges).items():
-                vstate[xi, py, dz] = value
-
         @pl.when(k < STEPS)
         def _():
             await_halo(frecv.at[p], fedges.at[p], f_recv_sem.at[p])
             await_halo(frecv.at[p], fedges.at[p], f_send_sem)
-            before = jnp.where(k > 0, half, 0.0)
             for (xi, py, dz), f in columns(fsend.at[p], frecv.at[p], fedges.at[p]).items():
-                vstate[xi, py, dz] = vstate[xi, py, dz] + before * f
+                vstate[xi, py, dz] = vstate[xi, py, dz] + half * f
                 held[xi, py, dz] = half * f
 
-        @pl.when(k > 0)
-        def _():
-            @pl.when(leads)
-            def _():
-                await_all(near_sums.at[p, pl.ds(0, n_near - 1)], near_send)
-                await_all(wide_sums.at[p, pl.ds(0, n_wide - 1)], wide_recv.at[p])
-
-            @pl.when(follows)
-            def _():
-                await_all(near_sums.at[p, pl.ds(0, n_near)], near_send)
-                await_all(wide_sums.at[p], wide_recv.at[p])
-
-            row = total_of(wide_sums, n_wide)
-
-            def across(low, high):
-                picked = jnp.where((row_lane >= low * quarter) & (row_lane < high * quarter), row, 0.0)
-                return jnp.broadcast_to(jnp.sum(picked, axis=1, keepdims=True), (1, lanes))
-
-            vigor, potential, count = across(0, 2), across(2, 3), across(3, 4)
-            square = (1.0 - BATH_STRENGTH) + (BATH_STRENGTH * GOAL_WARMTH * 1.5) * count / vigor
-            which = lax.broadcasted_iota(jnp.int32, (2, lanes), 1)
-            record = jnp.concatenate([potential, square * vigor], axis=0) / slot_total
-            history[...] = jnp.where(which == k - 1, record, history[...])
-            scale[...] = jnp.sqrt(square)
-
-            @pl.when(leads)
-            def _():
-                await_all(wide_out, wide_send)
-
-        lam = scale[...]
+        @pl.when(leads)
+        def _():
+            await_all(near_sums.at[p, pl.ds(0, n_near - 1)], near_send)
+            await_all(wide_sums.at[p, pl.ds(0, n_wide - 1)], wide_recv.at[p])
+
+        @pl.when(follows)
+        def _():
+            await_all(near_sums.at[p, pl.ds(0, n_near)], near_send)
+            await_all(wide_sums.at[p], wide_recv.at[p])
+
+        row = total_of(wide_sums, n_wide)
+
+        def across(low, high):
+            picked = jnp.where((row_lane >= low * quarter) & (row_lane < high * quarter), row, 0.0)
+            return jnp.broadcast_to(jnp.sum(picked, axis=1, keepdims=True), (1, lanes))
+
+        vigor, potential, count = across(0, 2), across(2, 3), across(3, 4)
+        square = (1.0 - BATH_STRENGTH) + (BATH_STRENGTH * GOAL_WARMTH * 1.5) * count / vigor
+        which = lax.broadcasted_iota(jnp.int32, (2, lanes), 1)
+        record = jnp.concatenate([potential, square * vigor], axis=0) / slot_total
+        history[...] = jnp.where(which == k - 1, record, history[...])
+
+        @pl.when(leads)
+        def _():
+            await_all(wide_out, wide_send)
+
+        lam = jnp.sqrt(square)
 
         @pl.when(k < STEPS)
         def _():
@@ -429,8 +521,7 @@
         return 0
 
     history[...] = jnp.zeros_like(history)
-    scale[...] = jnp.ones_like(scale)
-    lax.fori_loop(0, STEPS + 1, step, 0)
+    lax.fori_loop(1, STEPS + 1, step, 0)
     await_halo(orecv, oedges, o_sem.at[0])
     await_halo(vrecv, vedges, v_sem.at[0])
 
@@ -455,8 +546,9 @@
     nx, ny, nz, slots = occupied.shape
     lanes = nz * slots
     tile = lanes // slots
-    assert axes[2] > 2 and tile >= 3 * nx
+    assert axes[2] > 2 and tile >= 3 * nx and min(nx, ny) >= 2 and nz == 2 * (ny + 2)
     _, flats, rows = partners_of(axes, ny)
+    _, deep_flats, deep_rows = deep_places(axes, ny)
     nxo = len(offsets_of(axes[0]))
     n_near, n_wide = (len(chips_of(axes, group)) for group in (NEAR, WIDE))
     f32 = jnp.float32
@@ -483,7 +575,13 @@
             state,
             state,
             pltpu.VMEM((nx + 2, ny + 2, 3, 3, slots, lanes), f32),
-            *halo,
+            pltpu.VMEM((nxo, ny + 7, 3, tile, lanes), f32),
+            pltpu.VMEM((nx + 4, 3, 3, 3, slots, lanes), f32),
+            pltpu.VMEM((nxo, ny + 3, tile, lanes), f32),
+            pltpu.VMEM((ny, tile, lanes), f32),
+            pltpu.VMEM((deep_flats, tile, lanes), f32),
+            pltpu.VMEM((2, 2 * ny, 1, lanes), f32),
+            pltpu.VMEM((deep_rows, 1, lanes), f32),
             *halo,
             pltpu.VMEM((nx, ny, nz, slots), jnp.int32),
             pltpu.VMEM((2, ny, tile, lanes), f32),
@@ -492,7 +590,6 @@
             pltpu.VMEM((2, rows, 1, lanes), f32),
             pltpu.VMEM((1, lanes), f32),
             pltpu.VMEM((2, lanes), f32),
-            pltpu.VMEM((1, lanes), f32),
             pltpu.VMEM((1, lanes), f32),
             pltpu.VMEM((2, 2 * n_near, 1, lanes), f32),
             pltpu.VMEM((1, lanes), f32),

time: 61.5 us -> 60.4 us (0.982)
  Pallas kernels: 60.7 us -> 59.6 us
    pallas_call x1, Pallas kernels: 60 us -> 58.9 us  [shards(): pl.pallas_call(functools.partial(kernel, axes, (nx, ny, nz, slots)), name...]
where the time goes in v1:
time: 60.4 us; the launch traced here: 60.3 us
  Pallas kernels  59.6 us (99%)
  between operations  0.64 us (1%)
    pallas_call x1, Pallas kernels, shards(): pl.pallas_call(functools.partial(kernel, axes, (nx, ny, nz, slots)), name...  58.9 us

profile of v1, /device:TPU:1, one launch (start us, length us, event | category | flops | bytes accessed | tf_op | source)
XLA Modules:
  0.0 60.3 jit_solution(10168543247756652904)
XLA Ops:
  0.6 58.9 %verlet.1.result = f32[7,8,128]{2,1,0:T(8,128)S(1)} custom-call(f32[2,2,3,8,16]{4,3,2,1,0:T(8,128)} %bitcast.6, f32[2,2,3,8,16]{4,3,2,1,0:T(8,128)} %bitcast.7, s32[2,2,8,16]{3,2,1,0:T(8,128)} %occ_in.1), custom_call_target="tpu_custom_call" | custom-call | tf_op jit(solution)/shard_map/verlet/pallas_call | solution.py:565
  59.5 0.7 %unpack.1 = (f32[2,2,3,8,16]{4,3,2,1,0:T(8,128)}, f32[2,2,3,8,16]{4,3,2,1,0:T(8,128)}, f32[2,2,3,8,16]{4,3,2,1,0:T(8,128)}, f32[2,4]{1,0:T(2,128)}) custom-call(f32[7,8,128]{2,1,0:T(8,128)S(1)} %verlet.1.result), custom_call_target="tpu_custom_call" | custom-call | tf_op jit(solution)/shard_map/unpack/pallas_call | solution.py:616

commit v2 on v1

--- a/solution.py
+++ b/solution.py
@@ -90,9 +90,9 @@
 
 def kernel(
     axes, shape, o_in, v_in, occ_in, result,
-    planes_in, kept, ostate, vstate, held, near, around, first_near, first_force, osend, orecv, oedge, oedges, vsend, vrecv, vedge, vedges,
+    planes_in, kept, ostate, vstate, held, near, around, ends_of, first_near, first_force, osend, orecv, oedge, oedges, vsend, vrecv, vedge, vedges,
     occ_planes, fsend, frecv, fedge, fedges, tally, history, row_sum, near_sums, chip_sum, wide_sums, wide_out,
-    in_sem, o_sem, v_sem, f_send_sem, f_recv_sem, near_send, near_recv, wide_send, wide_recv,
+    in_sem, o_sem, o_recv_sem, v_sem, f_send_sem, f_recv_sem, near_send, near_recv, wide_send, wide_recv,
 ):
     gx, gy, gz = axes
     nx, ny, nz, slots = shape
@@ -155,7 +155,7 @@
 
     barrier = pltpu.get_barrier_semaphore()
 
-    greeted = [device(d) for d in partners]
+    greeted = [device(d) for d in reversed([*partners])]
     greeted += [member(d, 1, which) for group in (near_chips, wide_chips) for d in group if any(d.values()) for which in (0, 1)]
     greeted.append(member({}, 1, 1 - core))
     for to in greeted:
@@ -204,12 +204,7 @@
     quarter = lanes // 4
     row_lane = lane[:1]
 
-    def folded(row, times):
-        for i in range(times):
-            row = row + pltpu.roll(row, lanes >> (i + 1), 1)
-        return row
-
-    tally[...] = folded(jnp.sum(w_rows, axis=0, keepdims=True), 2)
+    tally[...] = jnp.broadcast_to(jnp.sum(w_rows, keepdims=True), (1, lanes))
 
     tile_lane = lax.broadcasted_iota(jnp.int32, (tile, lanes), 1)
     tile_row = lax.broadcasted_iota(jnp.int32, (tile, lanes), 0)
@@ -236,10 +231,10 @@
     for d, at in reversed([*places.items()]):
         to = device(tuple(-x for x in d))
         if d[2] == 0:
-            remote(osend, orecv.at[pl.ds(at, ny)], o_sem.at[0, 0], o_sem.at[1, 0], to).start()
+            remote(osend, orecv.at[pl.ds(at, ny)], o_sem.at[0], o_recv_sem.at[d[1] % 3, 0], to).start()
         else:
             src = oedge.at[0 if d[2] == 1 else 1]
-            remote(src, oedges.at[pl.ds(at, 2 * ny)], o_sem.at[0, 1], o_sem.at[1, 1], to).start()
+            remote(src, oedges.at[pl.ds(at, 2 * ny)], o_sem.at[1], o_recv_sem.at[d[1] % 3, 1], to).start()
     for copy in copies_of(vsend, vrecv, vedge, vedges, v_sem.at[0], v_sem.at[1]):
         copy.start()
 
@@ -268,23 +263,34 @@
     deep_x, deep_y = deep(gx, nx), deep(gy, ny)
     pairs = ny + 2
 
-    def neighbourhood():
-        ends_of = {}
+    def lay(xi, at, mid, below, above):
+        below, above = ([unpacked(oedges[e + depth]) for depth in range(2)] for e in (below, above))
+        low = jnp.where(tile_lane >= lanes - slots, below[0], mid)
+        high = jnp.where(tile_lane < slots, above[0], mid)
+        around[xi, at, 0] = pltpu.roll(low, slots, 1)
+        around[xi, at, 1] = mid
+        around[xi, at, 2] = pltpu.roll(high, lanes - slots, 1)
+        bottom = jnp.where(cell == 0, below[1], jnp.where(cell == 1, below[0], pltpu.roll(mid, 2 * slots, 1)))
+        top = jnp.where(cell == nz - 1, above[1], above[0])
+        top = jnp.where(cell == nz - 3, pltpu.roll(mid, lanes - 2 * slots, 1), top)
+        ends_of[xi, at] = jnp.where(cell < nz // 2, bottom, top)
+
+    def await_row(b, level_tiles):
+        await_all(orecv.at[pl.ds(0, level_tiles)], o_recv_sem.at[b, 0])
+        await_all(oedges.at[pl.ds(0, 4 * ny * len(xs))], o_recv_sem.at[b, 1])
+
+    def lay_beside(up):
+        await_row(2 - up, ny * len(xs))
         for xi, a in enumerate(xs):
-            for at, (b, yl) in enumerate(deep_y):
-                mid = osend[yl] if (a, b) == (0, 0) else orecv[places[a, b, 0] + yl]
-                below, above = (
-                    [unpacked(oedges[places[a, b, c] + 2 * yl + depth]) for depth in range(2)] for c in (-1, 1)
+            above, below = ([places[a, canonical(gy, b), c] for c in (0, -1, 1)] for b in (1, -1))
+            level_at, low_at, high_at = (m + up * (p - m) for p, m in zip(above, below))
+            for yl in range(2):
+                layer = (ny - 2) * (1 - up) + yl
+                lay(
+                    xi, yl + up * (ny + 2), orecv[level_at + layer], low_at + 2 * layer, high_at + 2 * layer
                 )
-                low = jnp.where(tile_lane >= lanes - slots, below[0], mid)
-                high = jnp.where(tile_lane < slots, above[0], mid)
-                around[xi, at, 0] = pltpu.roll(low, slots, 1)
-                around[xi, at, 1] = mid
-                around[xi, at, 2] = pltpu.roll(high, lanes - slots, 1)
-                bottom = jnp.where(cell == 0, below[1], jnp.where(cell == 1, below[0], pltpu.roll(mid, 2 * slots, 1)))
-                top = jnp.where(cell == nz - 1, above[1], above[0])
-                top = jnp.where(cell == nz - 3, pltpu.roll(mid, lanes - 2 * slots, 1), top)
-                ends_of[xi, at] = jnp.where(cell < nz // 2, bottom, top)
+
+    def lay_packed():
         for xi in range(len(xs)):
             for dy in range(3):
                 for dz in range(3):
@@ -295,13 +301,6 @@
                         taken = jnp.take_along_axis(ends_of[xi, t + dy], source, axis=1, mode="promise_in_bounds")
                         gathered = jnp.where(cell // 2 == t, taken, gathered)
                     around[xi, pairs + 2 + dy, dz] = gathered
-
-    await_halo(orecv, oedges, o_sem.at[1])
-    neighbourhood()
-    for xi in range(len(xs)):
-        for py in range(ny + 2):
-            for dz in range(3):
-                ostate[xi, py, dz] = around[xi, py + 1, dz]
 
     lane_id = lax.broadcasted_iota(jnp.int32, (slots, lanes), 1)
     slot_id = lax.broadcasted_iota(jnp.int32, (slots, lanes), 0)
@@ -368,7 +367,20 @@
         return 0
 
     first_force[...] = jnp.zeros_like(first_force)
-    lax.fori_loop(0, pairs + 1, first_row, 0)
+    await_row(0, ny * (len(xs) - 1))
+    for xi, a in enumerate(xs):
+        for yl in range(ny):
+            mid = osend[yl] if a == 0 else orecv[places[a, 0, 0] + yl]
+            lay(xi, yl + 2, mid, places[a, 0, -1] + 2 * yl, places[a, 0, 1] + 2 * yl)
+    lay_beside(1 - core)
+    near_rows = pairs // 2
+    lax.fori_loop(0, near_rows, lambda t, _: first_row(t + near_rows * (1 - core), 0), 0)
+    lay_beside(core)
+    lay_packed()
+    last = pairs - near_rows
+    lax.fori_loop(
+        0, last + 1, lambda t, _: first_row((t + near_rows * core) * (1 - t // last) + pairs * (t // last), 0), 0
+    )
 
     await_halo(vrecv, vedges, v_sem.at[1])
     first_v = columns(vsend, vrecv, vedges)
@@ -385,7 +397,7 @@
             for dz, f in enumerate((low, mid, high)):
                 v = first_v[xi, py, dz] + half * f
                 vstate[xi, py, dz] = v
-                ostate[xi, py, dz] = ostate[xi, py, dz] + TIME_STEP * v
+                ostate[xi, py, dz] = around[xi, py + 1, dz] + TIME_STEP * v
 
     def step(k, _):
         p = lax.rem(k, 2)
@@ -413,8 +425,8 @@
         for y in range(ny):
             v = vstate[0, y + 1, 1] + half * fsend[p, y]
             kinetic = kinetic + v * v
-        kinetic = folded(jnp.sum(kinetic, axis=0, keepdims=True), 1)
-        potential = folded(energy_rows, 2)
+        kinetic = jnp.sum(jnp.sum(kinetic, axis=0, keepdims=True), axis=1, keepdims=True)
+        potential = jnp.sum(energy_rows, axis=1, keepdims=True)
         row = jnp.where(
             row_lane < 2 * quarter, 0.5 * kinetic, jnp.where(row_lane < 3 * quarter, 0.5 * potential, tally[...])
         )
@@ -484,11 +496,10 @@
 
         row = total_of(wide_sums, n_wide)
 
-        def across(low, high):
-            picked = jnp.where((row_lane >= low * quarter) & (row_lane < high * quarter), row, 0.0)
-            return jnp.broadcast_to(jnp.sum(picked, axis=1, keepdims=True), (1, lanes))
-
-        vigor, potential, count = across(0, 2), across(2, 3), across(3, 4)
+        def across(part):
+            return jnp.full((1, lanes), row[0, part * quarter], jnp.float32)
+
+        vigor, potential, count = across(0), across(2), across(3)
         square = (1.0 - BATH_STRENGTH) + (BATH_STRENGTH * GOAL_WARMTH * 1.5) * count / vigor
         which = lax.broadcasted_iota(jnp.int32, (2, lanes), 1)
         record = jnp.concatenate([potential, square * vigor], axis=0) / slot_total
@@ -522,7 +533,7 @@
 
     history[...] = jnp.zeros_like(history)
     lax.fori_loop(1, STEPS + 1, step, 0)
-    await_halo(orecv, oedges, o_sem.at[0])
+    await_halo(orecv, oedges, o_sem)
     await_halo(vrecv, vedges, v_sem.at[0])
 
 
@@ -546,7 +557,7 @@
     nx, ny, nz, slots = occupied.shape
     lanes = nz * slots
     tile = lanes // slots
-    assert axes[2] > 2 and tile >= 3 * nx and min(nx, ny) >= 2 and nz == 2 * (ny + 2)
+    assert axes[2] > 2 and tile >= 3 * nx and min(nx, ny) >= 2 and ny % 2 == 0 and nz == 2 * (ny + 2)
     _, flats, rows = partners_of(axes, ny)
     _, deep_flats, deep_rows = deep_places(axes, ny)
     nxo = len(offsets_of(axes[0]))
@@ -576,6 +587,7 @@
             state,
             pltpu.VMEM((nx + 2, ny + 2, 3, 3, slots, lanes), f32),
             pltpu.VMEM((nxo, ny + 7, 3, tile, lanes), f32),
+            pltpu.VMEM((nxo, ny + 4, tile, lanes), f32),
             pltpu.VMEM((nx + 4, 3, 3, 3, slots, lanes), f32),
             pltpu.VMEM((nxo, ny + 3, tile, lanes), f32),
             pltpu.VMEM((ny, tile, lanes), f32),
@@ -596,7 +608,8 @@
             pltpu.VMEM((2, n_wide, 1, lanes), f32),
             pltpu.VMEM((2 * n_wide - 1, 1, lanes), f32),
             dma((3,)),
-            dma((2, 2)),
+            dma((2,)),
+            dma((3, 2)),
             dma((2, 2)),
             dma((2,)),
             dma((2, 2)),

time: 60.4 us -> 60.1 us (level)
  no operation moved by 1% of the time
where the time goes in v2:
time: 60.1 us; the launch traced here: 60 us
  Pallas kernels  59.3 us (99%)
  between operations  0.64 us (1%)
    pallas_call x1, Pallas kernels, shards(): pl.pallas_call(functools.partial(kernel, axes, (nx, ny, nz, slots)), name...  58.6 us

profile of v2, /device:TPU:1, one launch (start us, length us, event | category | flops | bytes accessed | tf_op | source)
XLA Modules:
  0.0 60.0 jit_solution(11309955020306279716)
XLA Ops:
  0.6 58.6 %verlet.1.result = f32[7,8,128]{2,1,0:T(8,128)S(1)} custom-call(f32[2,2,3,8,16]{4,3,2,1,0:T(8,128)} %bitcast.6, f32[2,2,3,8,16]{4,3,2,1,0:T(8,128)} %bitcast.7, s32[2,2,8,16]{3,2,1,0:T(8,128)} %occ_in.1), custom_call_target="tpu_custom_call" | custom-call | tf_op jit(solution)/shard_map/verlet/pallas_call | solution.py:576
  59.2 0.7 %unpack.1 = (f32[2,2,3,8,16]{4,3,2,1,0:T(8,128)}, f32[2,2,3,8,16]{4,3,2,1,0:T(8,128)}, f32[2,2,3,8,16]{4,3,2,1,0:T(8,128)}, f32[2,4]{1,0:T(2,128)}) custom-call(f32[7,8,128]{2,1,0:T(8,128)S(1)} %verlet.1.result), custom_call_target="tpu_custom_call" | custom-call | tf_op jit(solution)/shard_map/unpack/pallas_call | solution.py:629

commit v3 on v2

--- a/solution.py
+++ b/solution.py
@@ -91,8 +91,8 @@
 def kernel(
     axes, shape, o_in, v_in, occ_in, result,
     planes_in, kept, ostate, vstate, held, near, around, ends_of, first_near, first_force, osend, orecv, oedge, oedges, vsend, vrecv, vedge, vedges,
-    occ_planes, fsend, frecv, fedge, fedges, tally, history, row_sum, near_sums, chip_sum, wide_sums, wide_out,
-    in_sem, o_sem, o_recv_sem, v_sem, f_send_sem, f_recv_sem, near_send, near_recv, wide_send, wide_recv,
+    occ_planes, fsend, frecv, fedge, fedges, tally, history, row_sum, near_sums, chip_sum, wide_sums, measure,
+    in_sem, first_sem, o_recv_sem, v_sem, f_send_sem, f_recv_sem, sum_send, near_recv, wide_recv,
 ):
     gx, gy, gz = axes
     nx, ny, nz, slots = shape
@@ -140,18 +140,20 @@
             where = pl.ds(need[0], len(need))
             to = device(tuple(-x for x in d))
             if d[2] == 0:
-                copies.append(remote(send.at[where], recv.at[pl.ds(at, len(need))], send_sem.at[0], recv_sem.at[0], to))
+                copies.append(remote(send.at[where], recv.at[pl.ds(at, len(need))], send_sem, recv_sem, to))
             else:
                 src = edge.at[0 if d[2] == 1 else 1, where]
-                copies.append(remote(src, edges.at[pl.ds(at, len(need))], send_sem.at[1], recv_sem.at[1], to))
+                copies.append(remote(src, edges.at[pl.ds(at, len(need))], send_sem, recv_sem, to))
         return copies
 
     def await_all(ref, sem):
         pltpu.make_async_copy(ref, ref, sem).wait()
 
-    def await_halo(recv, edges, sem):
-        await_all(recv, sem.at[0])
-        await_all(edges, sem.at[1])
+    def await_rows(n, sem):
+        await_all(measure.at[pl.ds(0, n)], sem)
+
+    halo_rows = flats * tile + rows
+    deep_rows = sum(ny * tile if d[2] == 0 else 2 * ny for d in deep_places(axes, ny)[0])
 
     barrier = pltpu.get_barrier_semaphore()
 
@@ -164,7 +166,7 @@
     loads = [
         pltpu.make_async_copy(o_in, planes_in.at[0], in_sem.at[0]),
         pltpu.make_async_copy(occ_in, occ_planes, in_sem.at[1]),
-        pltpu.make_async_copy(v_in, planes_in.at[1], in_sem.at[2]),
+        pltpu.make_async_copy(v_in, planes_in.at[1], in_sem.at[0]),
     ]
     for load in loads:
         load.start()
@@ -182,8 +184,8 @@
         wide = wide.reshape(-1, nz, lanes)
         return jnp.sum(jnp.where((lane // slots == level)[None], wide, 0.0), axis=1)
 
-    for load in loads:
-        load.wait()
+    await_all(planes_in, in_sem.at[0])
+    loads[1].wait()
     o_rows = rows_of(planes_in[0])
     v_rows = rows_of(planes_in[1])
     w_rows = rows_of(occ_planes[...].astype(jnp.float32))
@@ -231,11 +233,11 @@
     for d, at in reversed([*places.items()]):
         to = device(tuple(-x for x in d))
         if d[2] == 0:
-            remote(osend, orecv.at[pl.ds(at, ny)], o_sem.at[0], o_recv_sem.at[d[1] % 3, 0], to).start()
+            remote(osend, orecv.at[pl.ds(at, ny)], first_sem, o_recv_sem.at[d[1] % 3], to).start()
         else:
             src = oedge.at[0 if d[2] == 1 else 1]
-            remote(src, oedges.at[pl.ds(at, 2 * ny)], o_sem.at[1], o_recv_sem.at[d[1] % 3, 1], to).start()
-    for copy in copies_of(vsend, vrecv, vedge, vedges, v_sem.at[0], v_sem.at[1]):
+            remote(src, oedges.at[pl.ds(at, 2 * ny)], first_sem, o_recv_sem.at[d[1] % 3], to).start()
+    for copy in copies_of(vsend, vrecv, vedge, vedges, first_sem, v_sem):
         copy.start()
 
     def columns(send, recv, edges):
@@ -276,8 +278,7 @@
         ends_of[xi, at] = jnp.where(cell < nz // 2, bottom, top)
 
     def await_row(b, level_tiles):
-        await_all(orecv.at[pl.ds(0, level_tiles)], o_recv_sem.at[b, 0])
-        await_all(oedges.at[pl.ds(0, 4 * ny * len(xs))], o_recv_sem.at[b, 1])
+        await_rows(level_tiles * tile + 4 * ny * len(xs), o_recv_sem.at[b])
 
     def lay_beside(up):
         await_row(2 - up, ny * len(xs))
@@ -382,7 +383,7 @@
         0, last + 1, lambda t, _: first_row((t + near_rows * core) * (1 - t // last) + pairs * (t // last), 0), 0
     )
 
-    await_halo(vrecv, vedges, v_sem.at[1])
+    await_rows(halo_rows, v_sem)
     first_v = columns(vsend, vrecv, vedges)
     for xi in range(len(xs)):
         outer = first_force[xi, pairs]
@@ -434,11 +435,11 @@
         at = index_in(NEAR) * 2 + core
         for d in near_chips:
             if any(d.values()):
-                remote(row_sum, near_sums.at[p, at], near_send, near_recv.at[p], member(d, -1, 1)).start()
+                remote(row_sum, near_sums.at[p, at], sum_send, near_recv.at[p], member(d, -1, 1)).start()
 
         @pl.when(follows)
         def _():
-            remote(row_sum, near_sums.at[p, at], near_send, near_recv.at[p], member({}, 1, 1)).start()
+            remote(row_sum, near_sums.at[p, at], sum_send, near_recv.at[p], member({}, 1, 1)).start()
 
         @pl.when(leads)
         def _():
@@ -472,26 +473,25 @@
                 for which in (0, 1):
                     if which == 0 or any(d.values()):
                         remote(
-                            chip_sum, wide_sums.at[p, at], wide_send, wide_recv.at[p], member(d, -1, which)
+                            chip_sum, wide_sums.at[p, at], sum_send, wide_recv.at[p], member(d, -1, which)
                         ).start()
             wide_sums[p, at] = row
 
         @pl.when(k < STEPS)
         def _():
-            await_halo(frecv.at[p], fedges.at[p], f_recv_sem.at[p])
-            await_halo(frecv.at[p], fedges.at[p], f_send_sem)
+            await_rows(halo_rows, f_recv_sem.at[p])
+            await_rows(halo_rows, f_send_sem)
             for (xi, py, dz), f in columns(fsend.at[p], frecv.at[p], fedges.at[p]).items():
                 vstate[xi, py, dz] = vstate[xi, py, dz] + half * f
                 held[xi, py, dz] = half * f
 
         @pl.when(leads)
         def _():
-            await_all(near_sums.at[p, pl.ds(0, n_near - 1)], near_send)
             await_all(wide_sums.at[p, pl.ds(0, n_wide - 1)], wide_recv.at[p])
 
         @pl.when(follows)
         def _():
-            await_all(near_sums.at[p, pl.ds(0, n_near)], near_send)
+            await_rows(n_near, sum_send)
             await_all(wide_sums.at[p], wide_recv.at[p])
 
         row = total_of(wide_sums, n_wide)
@@ -507,7 +507,7 @@
 
         @pl.when(leads)
         def _():
-            await_all(wide_out, wide_send)
+            await_rows(n_near + 2 * n_wide - 2, sum_send)
 
         lam = jnp.sqrt(square)
 
@@ -533,8 +533,7 @@
 
     history[...] = jnp.zeros_like(history)
     lax.fori_loop(1, STEPS + 1, step, 0)
-    await_halo(orecv, oedges, o_sem)
-    await_halo(vrecv, vedges, v_sem.at[0])
+    await_rows(deep_rows + halo_rows, first_sem)
 
 
 def unpack(shape, result, o_out, v_out, f_out, h_out):
@@ -606,16 +605,15 @@
             pltpu.VMEM((2, 2 * n_near, 1, lanes), f32),
             pltpu.VMEM((1, lanes), f32),
             pltpu.VMEM((2, n_wide, 1, lanes), f32),
-            pltpu.VMEM((2 * n_wide - 1, 1, lanes), f32),
+            pltpu.VMEM((deep_flats * tile + deep_rows + flats * tile + rows, 1, lanes), f32),
+            dma((2,)),
+            dma,
             dma((3,)),
-            dma((2,)),
-            dma((3, 2)),
-            dma((2, 2)),
-            dma((2,)),
-            dma((2, 2)),
+            dma,
             dma,
             dma((2,)),
             dma,
+            dma((2,)),
             dma((2,)),
         ],
         compiler_params=pltpu.CompilerParams(

time: 60.1 us -> 60 us (level)
  no operation moved by 1% of the time
where the time goes in v3:
time: 60 us; the launch traced here: 59.8 us
  Pallas kernels  59.2 us (99%)
  between operations  0.64 us (1%)
    pallas_call x1, Pallas kernels, shards(): pl.pallas_call(functools.partial(kernel, axes, (nx, ny, nz, slots)), name...  58.5 us

profile of v3, /device:TPU:1, one launch (start us, length us, event | category | flops | bytes accessed | tf_op | source)
XLA Modules:
  0.0 59.8 jit_solution(5289780881040242420)
XLA Ops:
  0.6 58.5 %verlet.1.result = f32[7,8,128]{2,1,0:T(8,128)S(1)} custom-call(f32[2,2,3,8,16]{4,3,2,1,0:T(8,128)} %bitcast.6, f32[2,2,3,8,16]{4,3,2,1,0:T(8,128)} %bitcast.7, s32[2,2,8,16]{3,2,1,0:T(8,128)} %occ_in.1), custom_call_target="tpu_custom_call" | custom-call | tf_op jit(solution)/shard_map/verlet/pallas_call | solution.py:575
  59.1 0.7 %unpack.1 = (f32[2,2,3,8,16]{4,3,2,1,0:T(8,128)}, f32[2,2,3,8,16]{4,3,2,1,0:T(8,128)}, f32[2,2,3,8,16]{4,3,2,1,0:T(8,128)}, f32[2,4]{1,0:T(2,128)}) custom-call(f32[7,8,128]{2,1,0:T(8,128)S(1)} %verlet.1.result), custom_call_target="tpu_custom_call" | custom-call | tf_op jit(solution)/shard_map/unpack/pallas_call | solution.py:627

commit v4 on v3

--- a/solution.py
+++ b/solution.py
@@ -22,8 +22,8 @@
 UNPACK_VMEM = 4 * 1024 * 1024
 
 
-NEAR = ("z",)
-WIDE = ("xl", "xh", "y")
+NEAR = ("xl", "xh", "y")
+WIDE = ("z",)
 
 
 def parts_of(axes):

time: 60 us -> 59.8 us (level)
  no operation moved by 1% of the time
where the time goes in v4:
time: 59.8 us; the launch traced here: 59.7 us
  Pallas kernels  59.1 us (99%)
  between operations  0.64 us (1%)
    pallas_call x1, Pallas kernels, shards(): pl.pallas_call(functools.partial(kernel, axes, (nx, ny, nz, slots)), name...  58.3 us

profile of v4, /device:TPU:1, one launch (start us, length us, event | category | flops | bytes accessed | tf_op | source)
XLA Modules:
  0.0 59.7 jit_solution(2206632132497651787)
XLA Ops:
  0.6 58.3 %verlet.1.result = f32[7,8,128]{2,1,0:T(8,128)S(1)} custom-call(f32[2,2,3,8,16]{4,3,2,1,0:T(8,128)} %bitcast.6, f32[2,2,3,8,16]{4,3,2,1,0:T(8,128)} %bitcast.7, s32[2,2,8,16]{3,2,1,0:T(8,128)} %occ_in.1), custom_call_target="tpu_custom_call" | custom-call | tf_op jit(solution)/shard_map/verlet/pallas_call | solution.py:575
  59.0 0.7 %unpack.1 = (f32[2,2,3,8,16]{4,3,2,1,0:T(8,128)}, f32[2,2,3,8,16]{4,3,2,1,0:T(8,128)}, f32[2,2,3,8,16]{4,3,2,1,0:T(8,128)}, f32[2,4]{1,0:T(2,128)}) custom-call(f32[7,8,128]{2,1,0:T(8,128)S(1)} %verlet.1.result), custom_call_target="tpu_custom_call" | custom-call | tf_op jit(solution)/shard_map/unpack/pallas_call | solution.py:627

commit v5 on v4

--- a/solution.py
+++ b/solution.py
@@ -91,7 +91,7 @@
 def kernel(
     axes, shape, o_in, v_in, occ_in, result,
     planes_in, kept, ostate, vstate, held, near, around, ends_of, first_near, first_force, osend, orecv, oedge, oedges, vsend, vrecv, vedge, vedges,
-    occ_planes, fsend, frecv, fedge, fedges, tally, history, row_sum, near_sums, chip_sum, wide_sums, measure,
+    occ_planes, fsend, frecv, fedge, fedges, tally, history, scale, row_sum, near_sums, chip_sum, wide_sums, measure,
     in_sem, first_sem, o_recv_sem, v_sem, f_send_sem, f_recv_sem, sum_send, near_recv, wide_recv,
 ):
     gx, gy, gz = axes
@@ -396,12 +396,19 @@
                 pltpu.roll(mid, lanes - slots, 1),
             )
             for dz, f in enumerate((low, mid, high)):
-                v = first_v[xi, py, dz] + half * f
-                vstate[xi, py, dz] = v
-                ostate[xi, py, dz] = around[xi, py + 1, dz] + TIME_STEP * v
+                vstate[xi, py, dz] = first_v[xi, py, dz]
+                held[xi, py, dz] = half * f
+                ostate[xi, py, dz] = around[xi, py + 1, dz]
 
     def step(k, _):
         p = lax.rem(k, 2)
+        lam = scale[...]
+        for xi in range(len(xs)):
+            for py in range(ny + 2):
+                for dz in range(3):
+                    v = vstate[xi, py, dz] * lam + held[xi, py, dz]
+                    vstate[xi, py, dz] = v
+                    ostate[xi, py, dz] = ostate[xi, py, dz] + TIME_STEP * v
         for py in range(ny + 2):
             nearby(py)
 
@@ -509,30 +516,18 @@
         def _():
             await_rows(n_near + 2 * n_wide - 2, sum_send)
 
-        lam = jnp.sqrt(square)
-
-        @pl.when(k < STEPS)
-        def _():
-            for xi in range(len(xs)):
-                for py in range(ny + 2):
-                    for dz in range(3):
-                        v = vstate[xi, py, dz] * lam + held[xi, py, dz]
-                        vstate[xi, py, dz] = v
-                        ostate[xi, py, dz] = ostate[xi, py, dz] + TIME_STEP * v
-
-        @pl.when(k == STEPS)
-        def _():
-            for y in range(ny):
-                here = ostate[0, y + 1, 1]
-                result[y] = jnp.where(here < 0.5 * FAR, here, kept[y])
-                result[ny + y] = (vstate[0, y + 1, 1] + half * fsend[p, y]) * lam
-                result[2 * ny + y] = fsend[p, y]
-            result[3 * ny, 0:2] = history[...]
-
+        scale[...] = jnp.sqrt(square)
         return 0
 
     history[...] = jnp.zeros_like(history)
+    scale[...] = jnp.ones_like(scale)
     lax.fori_loop(1, STEPS + 1, step, 0)
+    for y in range(ny):
+        here = ostate[0, y + 1, 1]
+        result[y] = jnp.where(here < 0.5 * FAR, here, kept[y])
+        result[ny + y] = (vstate[0, y + 1, 1] + half * fsend[STEPS % 2, y]) * scale[...]
+        result[2 * ny + y] = fsend[STEPS % 2, y]
+    result[3 * ny, 0:2] = history[...]
     await_rows(deep_rows + halo_rows, first_sem)
 
 
@@ -602,6 +597,7 @@
             pltpu.VMEM((1, lanes), f32),
             pltpu.VMEM((2, lanes), f32),
             pltpu.VMEM((1, lanes), f32),
+            pltpu.VMEM((1, lanes), f32),
             pltpu.VMEM((2, 2 * n_near, 1, lanes), f32),
             pltpu.VMEM((1, lanes), f32),
             pltpu.VMEM((2, n_wide, 1, lanes), f32),

time: 59.8 us -> 59.9 us (level)
  no operation moved by 1% of the time
where the time goes in v5:
time: 59.9 us; the launch traced here: 59.8 us
  Pallas kernels  59.2 us (99%)
  between operations  0.64 us (1%)
    pallas_call x1, Pallas kernels, shards(): pl.pallas_call(functools.partial(kernel, axes, (nx, ny, nz, slots)), name...  58.4 us

profile of v5, /device:TPU:1, one launch (start us, length us, event | category | flops | bytes accessed | tf_op | source)
XLA Modules:
  0.0 59.8 jit_solution(12203393280565279433)
XLA Ops:
  0.6 58.4 %verlet.1.result = f32[7,8,128]{2,1,0:T(8,128)S(1)} custom-call(f32[2,2,3,8,16]{4,3,2,1,0:T(8,128)} %bitcast.6, f32[2,2,3,8,16]{4,3,2,1,0:T(8,128)} %bitcast.7, s32[2,2,8,16]{3,2,1,0:T(8,128)} %occ_in.1), custom_call_target="tpu_custom_call" | custom-call | tf_op jit(solution)/shard_map/verlet/pallas_call | solution.py:570
  59.1 0.7 %unpack.1 = (f32[2,2,3,8,16]{4,3,2,1,0:T(8,128)}, f32[2,2,3,8,16]{4,3,2,1,0:T(8,128)}, f32[2,2,3,8,16]{4,3,2,1,0:T(8,128)}, f32[2,4]{1,0:T(2,128)}) custom-call(f32[7,8,128]{2,1,0:T(8,128)S(1)} %verlet.1.result), custom_call_target="tpu_custom_call" | custom-call | tf_op jit(solution)/shard_map/unpack/pallas_call | solution.py:623

commit v6 on v4

--- a/solution.py
+++ b/solution.py
@@ -158,10 +158,16 @@
     barrier = pltpu.get_barrier_semaphore()
 
     greeted = [device(d) for d in reversed([*partners])]
-    greeted += [member(d, 1, which) for group in (near_chips, wide_chips) for d in group if any(d.values()) for which in (0, 1)]
+    others = [d for group in (near_chips, wide_chips) for d in group if any(d.values())]
+    greeted += [member(d, 1, 1) for d in others]
     greeted.append(member({}, 1, 1 - core))
     for to in greeted:
         pl.semaphore_signal(barrier, inc=1, device_id=to, device_id_type=MESH)
+
+    @pl.when(leads)
+    def _():
+        for d in others:
+            pl.semaphore_signal(barrier, inc=1, device_id=member(d, 1, 0), device_id_type=MESH)
 
     loads = [
         pltpu.make_async_copy(o_in, planes_in.at[0], in_sem.at[0]),
@@ -228,7 +234,7 @@
                 oedge[side, 2 * y + depth] = packed(osend[y], side, depth)
             vedge[side, y] = packed(vsend[y], side)
 
-    pl.semaphore_wait(barrier, len(greeted))
+    pl.semaphore_wait(barrier, len(greeted) + len(others) * core)
     places, _, _ = deep_places(axes, ny)
     for d, at in reversed([*places.items()]):
         to = device(tuple(-x for x in d))

time: 59.8 us -> 59.5 us (level)
  no operation moved by 1% of the time
where the time goes in v6:
time: 59.5 us; the launch traced here: 59.4 us
  Pallas kernels  58.7 us (99%)
  between operations  0.64 us (1%)
    pallas_call x1, Pallas kernels, shards(): pl.pallas_call(functools.partial(kernel, axes, (nx, ny, nz, slots)), name...  58 us

profile of v6, /device:TPU:1, one launch (start us, length us, event | category | flops | bytes accessed | tf_op | source)
XLA Modules:
  0.0 59.4 jit_solution(1768660109883834126)
XLA Ops:
  0.6 58.0 %verlet.1.result = f32[7,8,128]{2,1,0:T(8,128)S(1)} custom-call(f32[2,2,3,8,16]{4,3,2,1,0:T(8,128)} %bitcast.6, f32[2,2,3,8,16]{4,3,2,1,0:T(8,128)} %bitcast.7, s32[2,2,8,16]{3,2,1,0:T(8,128)} %occ_in.1), custom_call_target="tpu_custom_call" | custom-call | tf_op jit(solution)/shard_map/verlet/pallas_call | solution.py:581
  58.6 0.7 %unpack.1 = (f32[2,2,3,8,16]{4,3,2,1,0:T(8,128)}, f32[2,2,3,8,16]{4,3,2,1,0:T(8,128)}, f32[2,2,3,8,16]{4,3,2,1,0:T(8,128)}, f32[2,4]{1,0:T(2,128)}) custom-call(f32[7,8,128]{2,1,0:T(8,128)S(1)} %verlet.1.result), custom_call_target="tpu_custom_call" | custom-call | tf_op jit(solution)/shard_map/unpack/pallas_call | solution.py:633
